TPU v7x, 32 devices: a 4x2x2 block of a 4x4x8 slice. The times are simulated.
32 devices in a mesh: data: 4 (over y, z), tp: 8 (over x, core).
Axes of the slice: x: 4, y: 2, z: 2, core: 2. Of those that a mesh axis runs over, the one named last changes fastest.
The devices are a block of a 4x4x8 slice.
Arguments:
- x: bfloat16 [16384, 14336], P('data', 'tp'), parts along dimension 0
- w: bfloat16 [14336, 4096], P('tp')
- r: bfloat16 [16384, 4096], P('data'), parts along dimension 0
- g: bfloat16 [4096], replicated
Outputs:
- output: bfloat16 [16384, 4096], P('data'), parts along dimension 0
There are 4 independent parts. A program takes and returns all parts, laid end to end along the dimension named above; an argument that names none is the same for every part.
All inputs are finite; a program needn't handle non-finite values.
Results may differ from a plain program's by a relative error of at most 0.0108178.
Values are sent between devices in bfloat16 or wider.
A program may use at most 768 MiB of HBM per device.

v0:
```python
import jax
import jax.numpy as jnp
from jax import lax
from jax.sharding import PartitionSpec as P

EPS = 1e-6


def solution(mesh):
    tp = mesh.shape["tp"]

    def local(x, w, r, g):
        rows = x.shape[0] // tp
        idx = lax.axis_index("tp")
        p = jnp.dot(x, w, preferred_element_type=jnp.float32).astype(jnp.bfloat16)
        y = lax.psum_scatter(p, "tp", scatter_dimension=0, tiled=True)
        rr = lax.dynamic_slice_in_dim(r, idx * rows, rows, axis=0)
        a = rr.astype(jnp.float32) + y.astype(jnp.float32)
        ms = jnp.mean(a * a, axis=-1, keepdims=True)
        zl = (a * lax.rsqrt(ms + EPS) * g.astype(jnp.float32)).astype(jnp.bfloat16)
        return lax.all_gather(zl, "tp", axis=0, tiled=True)

    return jax.shard_map(
        local,
        mesh=mesh,
        in_specs=(P("data", "tp"), P("tp", None), P("data", None), P(None)),
        out_specs=P("data", None),
        check_vma=False,
    )
```

profile of v0, /device:TPU:81, one launch (start us, length us, event | category | flops | bytes accessed | tf_op | source)
XLA Modules:
  0.0 442.8 jit_solution(2024471993453397546)
XLA Ops:
  6.5 0.0 reduce-scatter.2.cloned.1.call-start
  6.6 69.4 %convolution_convert_fusion = bf16[4096,4096]{1,0:T(8,128)(2,1)} fusion(bf16[4096,1792]{1,0:T(8,128)(2,1)} %param.4, bf16[1792,4096]{1,0:T(8,128)(2,1)} %param.5), kind=kOutput, calls=%fused_computation | convolution fusion | flops 60146319360 | bytes 62914560 | tf_op jit(solution)/shard_map/dot_general | solution.py:15
  75.9 0.0 copy-start.1
  75.9 0.1 reduce-scatter.2.cloned.1.call-update
  76.0 0.2 all-gather.2.cloned.1.call-start
  76.3 0.4 copy-done.1
  76.6 170.6 %reduce-scatter.2.cloned.1.call-done = bf16[512,4096]{1,0:T(8,128)(2,1)} async-done(((bf16[4096,4096]{1,0:T(8,128)(2,1)}), bf16[512,4096]{1,0:T(8,128)(2,1)}) %reduce-scatter.2.cloned.1.call-update) | async-done | bytes 4194320 | tf_op jit(solution)/shard_map/reduce_scatter | solution.py:16
  247.2 0.0 copy-start
  247.2 5.0 %multiply_reduce_fusion = f32[512]{0:T(512)S(1)} fusion(bf16[512,4096]{1,0:T(8,128)(2,1)} %reduce-scatter.2.cloned.1.call-done, bf16[4096,4096]{1,0:T(8,128)(2,1)} %param.6, s32[]{:T(128)S(6)} %select_n.3), kind=kLoop, calls=%fused_computation.2 | loop fusion | flops 10485248 | bytes 8390660 | tf_op jit(solution)/shard_map/reduce_sum | solution.py:19
  252.3 0.0 copy-done
  252.3 6.4 %multiply_convert_fusion = bf16[512,4096]{1,0:T(8,128)(2,1)} fusion(bf16[512,4096]{1,0:T(8,128)(2,1)S(1)} %copy-done, f32[4096]{0:T(1024)S(1)} %convert_element_type.18, f32[512]{0:T(512)S(1)} %add_rsqrt_fusion, bf16[4096,4096]{1,0:T(8,128)(2,1)} %param.6, s32[]{:T(128)S(6)} %select_n.3), kind=kLoop, calls=%fused_computation.1 | loop fusion | flops 12582912 | bytes 12601348 | tf_op jit(solution)/shard_map/convert_element_type | solution.py:20
  258.7 0.1 all-gather.2.cloned.1.call-update
  258.8 154.3 %all-gather.2.cloned.1.call-done = bf16[4096,4096]{1,0:T(8,128)(2,1)} async-done(((bf16[512,4096]{1,0:T(8,128)(2,1)}), bf16[4096,4096]{1,0:T(8,128)(2,1)}) %all-gather.2.cloned.1.call-update) | async-done | bytes 33554448 | tf_op jit(solution)/shard_map/all_gather | solution.py:21
  413.1 22.9 %copy.6 = bf16[4096,4096]{1,0:T(8,128)(2,1)} copy(bf16[4096,4096]{1,0:T(8,128)(2,1)} %all-gather.2.cloned.1.call-done) | data formatting | bytes 67108864
  (2 shorter events, 0.0 us)
Async XLA Ops:
  6.5 240.7 %reduce-scatter.2.cloned.1.call-start = ((), (), s32[]{:S(2)}) async-start(), calls=%async_computation.1 | async-start | bytes 37748736 | tf_op jit(solution)/shard_map/reduce_scatter | solution.py:16
  75.9 0.7 copy-start.1
  76.0 337.1 %all-gather.2.cloned.1.call-start = ((), (), s32[]{:S(2)}) async-start(), calls=%async_computation.2 | async-start | bytes 37748736 | tf_op jit(solution)/shard_map/all_gather | solution.py:21
  247.2 5.0 %copy-start = (bf16[512,4096]{1,0:T(8,128)(2,1)S(1)}, bf16[512,4096]{1,0:T(8,128)(2,1)}, u32[]{:S(2)}) copy-start(bf16[512,4096]{1,0:T(8,128)(2,1)} %reduce-scatter.2.cloned.1.call-done) | copy-start | bytes 12582916
Sparse Core Ops, SparseCore 0:
  76.1 171.0 reduce-scatter.1
  258.9 154.1 all-gather.1
where the time goes:
time: 443 us
  waiting for transfers between devices  325 us (73%)
  matrix products  69.4 us (16%)
  local copies, waits for them, and re-layouts  23.3 us (5%)
  between operations  13.4 us (3%)
  other arithmetic  11.4 us (3%)
    reduce_scatter x1, waiting for transfers between devices, local(): y = lax.psum_scatter(p, 'tp', scatter_dimension=0, tiled=True)  171 us
    all_gather x1, waiting for transfers between devices, local(): return lax.all_gather(zl, 'tp', axis=0, tiled=True)  154 us
    dot_general x1, matrix products, local(): p = jnp.dot(x, w, preferred_element_type=jnp.float32).astype(jnp.bfloat16)  69.4 us
    unnamed x5, local copies, waits for them, and re-layouts  23.3 us
  transfers between devices with their start and end apart: 2, of which 2 were waited for; matrix products, arithmetic and copies ran while one was open for 0% of the time, Pallas kernels for 0%

commit v1 on v0

v1 whole, which is shorter than its diff:
```python
import functools

import jax
import jax.numpy as jnp
from jax import lax
from jax.experimental import pallas as pl
from jax.experimental.pallas import tpu as pltpu
from jax.sharding import PartitionSpec as P

EPS = 1e-6
MESH = pl.DeviceIdType.MESH
NC = 4
NS = 4


def kernel(
    tp, x, w, r, g, out,
    xbuf, wbuf, gbuf, rbuf, stage, part, recv,
    x_sem, w_sem, g_sem, pair_s, pair_r, rs_s, rs_r, cb_s, cb_r,
    ag_s, ag_r, fw_s, fw_r, sib_s, sib_r, loc_s,
):
    n = tp // 2
    blk = part.shape[1]
    cols = wbuf.shape[2]
    sub = blk // NS
    me = lax.axis_index("tp")
    chip = me // 2
    core = me - 2 * chip
    sib = 2 * chip + 1 - core

    def chip_at(d):
        return lax.rem(chip + d + n, n)

    right = 2 * chip_at(1) + core
    left = 2 * chip_at(-1) + core

    def row_of(q, k, o):
        return pl.multiple_of(blk * (4 * q + 2 * k + o), blk)

    def remote(src, dst, ss, rs, dev):
        return pltpu.make_async_remote_copy(
            src_ref=src, dst_ref=dst, send_sem=ss, recv_sem=rs,
            device_id={"tp": dev}, device_id_type=MESH,
        )

    def load_x(pair):
        res = []
        for side in range(2):
            sign = 1 - 2 * side
            q = chip_at(sign * ((4 - pair) // 2))
            o = lax.rem(side + 1 + pair, 2)
            for which in range(2):
                k = core if which == 0 else 1 - core
                slot = lax.rem(pair, 2)
                res.append(pltpu.make_async_copy(
                    x.at[pl.ds(row_of(q, k, o), blk), :],
                    xbuf.at[slot, 2 * side + which],
                    x_sem.at[slot, 2 * side + which],
                ))
        return res

    def load_w(c):
        return pltpu.make_async_copy(
            w.at[:, pl.ds(pl.multiple_of(c * cols, cols), cols)], wbuf.at[c], w_sem.at[c]
        )

    def col(c):
        return pl.ds(pl.multiple_of(c * cols, cols), cols)

    def row(s):
        return pl.ds(pl.multiple_of(s * sub, sub), sub)

    for cp in load_x(0):
        cp.start()
    for c in range(NC):
        load_w(c).start()
    for cp in load_x(1):
        cp.start()
    own0 = row_of(chip, core, 0)
    load_r = pltpu.make_async_copy(r.at[pl.ds(own0, 2 * blk), :], rbuf, g_sem.at[0])
    load_g = pltpu.make_async_copy(g, gbuf, g_sem.at[1])
    load_r.start()
    load_g.start()

    barrier = pltpu.get_barrier_semaphore()
    for dev in (sib, left, right):
        pl.semaphore_signal(barrier, inc=1, device_id={"tp": dev}, device_id_type=MESH)
    pl.semaphore_wait(barrier, 3)

    per = 2 * NC
    steps = 4 * per

    def split(t):
        pair = t // per
        c = (t - pair * per) // 2
        side = t - 2 * (t // 2)
        return pair, c, side

    def pair_copy(t):
        pair, c, side = split(t)
        return remote(
            stage.at[lax.rem(t, 4)], part.at[2 * pair + side, :, col(c)],
            pair_s.at[lax.rem(t, 4)], pair_r.at[t], sib,
        )

    def rs_copy(t):
        pair, c, side = split(t)
        job = 2 * pair + side
        return remote(
            part.at[job, :, col(c)], recv.at[job, :, col(c)],
            rs_s.at[t], rs_r.at[t], jnp.where(side == 0, right, left),
        )

    def product(pair, side, which, c):
        return jnp.dot(
            xbuf[lax.rem(pair, 2), 2 * side + which], wbuf[c],
            preferred_element_type=jnp.float32,
        )

    @pl.loop(0, steps + 1)
    def _(t):
        @pl.when(t < steps)
        def _():
            pair, c, side = split(t)

            @pl.when(lax.rem(t, per) == 0)
            def _():
                for cp in load_x(pair):
                    cp.wait()

            @pl.when(jnp.logical_and(t < per, side == 0))
            def _():
                load_w(c).wait()

            @pl.when(t >= 4)
            def _():
                pair_copy(t - 4).wait_send()

            stage[lax.rem(t, 4)] = product(pair, side, 1, c).astype(jnp.bfloat16)
            pair_copy(t).start()

        @pl.when(t > 0)
        def _():
            u = t - 1
            pair, c, side = split(u)
            job = 2 * pair + side
            pair_copy(u).wait_recv()
            acc = product(pair, side, 0, c)
            acc = acc + part[job, :, col(c)].astype(jnp.float32)
            part[job, :, col(c)] = acc.astype(jnp.bfloat16)

            @pl.when(u < 2 * per)
            def _():
                rs_copy(u).start()

            @pl.when(jnp.logical_and(lax.rem(u, per) == per - 1, pair < 2))
            def _():
                for cp in load_x(pair + 2):
                    cp.start()

    def cb_copy(i):
        s = i // 2
        side = i - 2 * s
        return remote(
            part.at[4 + side, row(s), :], recv.at[4 + side, row(s), :],
            cb_s.at[i], cb_r.at[i], jnp.where(side == 0, right, left),
        )

    @pl.loop(0, per)
    def _(t):
        rs_copy(t).wait_recv()

    @pl.loop(0, 2 * NS)
    def _(i):
        s = i // 2
        side = i - 2 * s
        total = part[4 + side, row(s), :].astype(jnp.float32)
        total = total + recv[side, row(s), :].astype(jnp.float32)
        part[4 + side, row(s), :] = total.astype(jnp.bfloat16)
        cb_copy(i).start()

    @pl.loop(per, 2 * per)
    def _(t):
        rs_copy(t).wait_recv()

    load_r.wait()
    load_g.wait()

    def out_rows(q, o, s, k=None):
        k = core if k is None else k
        return out.at[pl.ds(pl.multiple_of(row_of(q, k, o) + s * sub, sub), sub), :]

    def ag_copy(i, d):
        s = i // 2
        o = i - 2 * s
        return remote(
            part.at[6 + o, row(s), :], out_rows(chip, o, s),
            ag_s.at[d, i], ag_r.at[d, i], right if d == 0 else left,
        )

    def own_sib(i):
        s = i // 2
        o = i - 2 * s
        return remote(
            part.at[6 + o, row(s), :], out_rows(chip, o, s),
            sib_s.at[0, i], sib_r.at[0, i], sib,
        )

    def own_out(i):
        s = i // 2
        o = i - 2 * s
        return pltpu.make_async_copy(part.at[6 + o, row(s), :], out_rows(chip, o, s), loc_s.at[i])

    grp = 16 if sub % 16 == 0 else sub

    @pl.loop(0, 2 * NS)
    def _(i):
        s = i // 2
        o = i - 2 * s
        cb_copy(2 * s + 1 - o).wait_recv()

        @pl.loop(0, sub // grp)
        def _(b):
            rows = pl.ds(pl.multiple_of(s * sub + b * grp, grp), grp)
            y = part[6 + o, rows, :].astype(jnp.float32)
            y = y + recv[2 + o, rows, :].astype(jnp.float32)
            y = y + recv[5 - o, rows, :].astype(jnp.float32)
            rr = rbuf[pl.ds(pl.multiple_of(o * blk + s * sub + b * grp, grp), grp), :]
            a = rr.astype(jnp.float32) + y.astype(jnp.bfloat16).astype(jnp.float32)
            ms = jnp.mean(a * a, axis=-1, keepdims=True)
            z = a * lax.rsqrt(ms + EPS) * gbuf[...].astype(jnp.float32)
            part[6 + o, rows, :] = z.astype(jnp.bfloat16)

        ag_copy(i, 0).start()
        ag_copy(i, 1).start()
        own_sib(i).start()
        own_out(i).start()

    def sib_copy(d, i):
        s = i // 2
        o = i - 2 * s
        rows = out_rows(chip_at(-1 if d == 0 else 1), o, s)
        return remote(rows, rows, sib_s.at[1 + d, i], sib_r.at[1 + d, i], sib)

    def fw_copy(d, s):
        rows = out_rows(chip_at(-1 if d == 0 else 1), d, s)
        return remote(rows, rows, fw_s.at[d, s], fw_r.at[d, s], right if d == 0 else left)

    def fw_sib(d, s):
        rows = out_rows(chip_at(2), d, s)
        return remote(rows, rows, sib_s.at[3, 2 * s + d], sib_r.at[3, 2 * s + d], sib)

    @pl.loop(0, NS)
    def _(s):
        for o in range(2):
            i = 2 * s + o
            for d in range(2):
                ag_copy(i, d).wait_recv()
                if o == d:
                    fw_copy(d, s).start()
                sib_copy(d, i).start()

    @pl.loop(0, NS)
    def _(s):
        for d in range(2):
            rows = out_rows(chip_at(2), d, s)
            remote(rows, rows, fw_s.at[d, s], fw_r.at[d, s], sib).wait_recv()
            fw_sib(d, s).start()

    @pl.loop(steps - 4, steps)
    def _(t):
        pair_copy(t).wait_send()

    @pl.loop(0, 2 * per)
    def _(t):
        rs_copy(t).wait_send()

    @pl.loop(0, 2 * NS)
    def _(i):
        cb_copy(i).wait_send()
        own_out(i).wait()
        own_sib(i).wait()
        for d in range(2):
            ag_copy(i, d).wait_send()
            sib_copy(d, i).wait()

    @pl.loop(0, NS)
    def _(s):
        for d in range(2):
            fw_copy(d, s).wait_send()
            fw_sib(d, s).wait()


def solution(mesh):
    tp = mesh.shape["tp"]

    def local(x, w, r, g):
        t, f = x.shape
        h = w.shape[1]
        blk = t // (2 * tp)
        dma = pltpu.SemaphoreType.DMA
        bf16 = jnp.bfloat16
        any_spec = pl.BlockSpec(memory_space=pl.ANY)
        return pl.pallas_call(
            functools.partial(kernel, tp),
            out_shape=jax.ShapeDtypeStruct((t, h), bf16),
            in_specs=[any_spec] * 4,
            out_specs=any_spec,
            scratch_shapes=[
                pltpu.VMEM((2, 4, blk, f), bf16),
                pltpu.VMEM((NC, f, h // NC), bf16),
                pltpu.VMEM((1, h), bf16),
                pltpu.VMEM((2 * blk, h), bf16),
                pltpu.VMEM((4, blk, h // NC), bf16),
                pltpu.VMEM((8, blk, h), bf16),
                pltpu.VMEM((6, blk, h), bf16),
                dma((2, 4)), dma((NC,)), dma((2,)),
                dma((4,)), dma((8 * NC,)),
                dma((4 * NC,)), dma((4 * NC,)),
                dma((2 * NS,)), dma((2 * NS,)),
                dma((2, 2 * NS)), dma((2, 2 * NS)),
                dma((2, NS)), dma((2, NS)),
                dma((4, 2 * NS)), dma((4, 2 * NS)),
                dma((2 * NS,)),
            ],
            compiler_params=pltpu.CompilerParams(
                collective_id=0, has_side_effects=True, vmem_limit_bytes=67043328,
            ),
            cost_estimate=pl.CostEstimate(
                flops=2 * t * f * h, bytes_accessed=2 * (t * f + f * h + 3 * t * h), transcendentals=0
            ),
        )(x, w, r, g.reshape(1, h))

    return jax.shard_map(
        local,
        mesh=mesh,
        in_specs=(P("data", "tp"), P("tp", None), P("data", None), P(None)),
        out_specs=P("data", None),
        check_vma=False,
    )
```

time: 443 us -> 311 us (0.70)
  waiting for transfers between devices: 325 us -> 0 us
  Pallas kernels: 0 us -> 287 us
  matrix products: 69.4 us -> 0 us
  between operations: 13.4 us -> 0.01 us
  other arithmetic: 11.4 us -> 0 us
    pallas_call x0 -> x1, Pallas kernels: none -> 287 us  [local(): pl.pallas_call(functools.partial(kernel, tp), out_shape=jax.ShapeDtypeStr...]
    reduce_scatter x1 -> x0, waiting for transfers between devices: 171 us -> none  [local(): y = lax.psum_scatter(p, 'tp', scatter_dimension=0, tiled=True)]
    all_gather x1 -> x0, waiting for transfers between devices: 154 us -> none  [local(): return lax.all_gather(zl, 'tp', axis=0, tiled=True)]
    dot_general x1 -> x0, matrix products: 69.4 us -> none  [local(): p = jnp.dot(x, w, preferred_element_type=jnp.float32).astype(jnp.bfloat16)]
    convert_element_type x2 -> x0, other arithmetic: 6.41 us -> none  [local(): zl = (a * lax.rsqrt(ms + EPS) * g.astype(jnp.float32)).astype(jnp.bfloat16)]
    reduce_sum x1 -> x0, other arithmetic: 5.03 us -> none  [local(): ms = jnp.mean(a * a, axis=-1, keepdims=True)]
    unnamed x5 -> x1, local copies, waits for them, and re-layouts: 23.3 us -> 22.9 us
  transfers between devices with their start and end apart: 2 -> 0, of which waited for: 2 -> 0; matrix products, arithmetic and copies ran while one was open for 0% -> 0% of each run, Pallas kernels for 0% -> 0%
where the time goes in v1:
time: 311 us
  Pallas kernels  287 us (92%)
  local copies, waits for them, and re-layouts  24.2 us (8%)
    pallas_call x1, Pallas kernels, local(): pl.pallas_call(functools.partial(kernel, tp), out_shape=jax.ShapeDtypeStr...  287 us
    unnamed x1, local copies, waits for them, and re-layouts  22.9 us

profile of v1, /device:TPU:81, one launch (start us, length us, event | category | flops | bytes accessed | tf_op | source)
XLA Modules:
  0.0 310.7 jit_solution(9684512531244977410)
XLA Ops:
  0.0 1.3 reshape.3.g
  1.3 286.5 %shard_map.46 = bf16[4096,4096]{1,0:T(8,128)(2,1)} custom-call(bf16[4096,1792]{1,0:T(8,128)(2,1)} %x.1, bf16[1792,4096]{1,0:T(8,128)(2,1)} %w.1, bf16[4096,4096]{1,0:T(8,128)(2,1)} %r.1, bf16[1,4096]{1,0:T(2,128)(2,1)} %reshape.3.g), custom_call_target="tpu_custom_call" | custom-call | flops 60129542144 | bytes 130023424 | tf_op jit(solution)/shard_map/pallas_call | solution.py:304
  287.8 22.9 %copy.6 = bf16[4096,4096]{1,0:T(8,128)(2,1)} copy(bf16[4096,4096]{1,0:T(8,128)(2,1)} %shard_map.46) | data formatting | bytes 67108864

commit v2 on v1

--- a/solution.py
+++ b/solution.py
@@ -11,16 +11,18 @@
 MESH = pl.DeviceIdType.MESH
 NC = 4
 NS = 4
+VMEM_COMM = 30 * 1024 * 1024
+VMEM_WRITE = 1024 * 1024
 
 
 def kernel(
     tp, x, w, r, g, out,
-    xbuf, wbuf, gbuf, rbuf, stage, part, recv,
+    xbuf, wbuf, gbuf, rbuf, stage,
     x_sem, w_sem, g_sem, pair_s, pair_r, rs_s, rs_r, cb_s, cb_r,
-    ag_s, ag_r, fw_s, fw_r, sib_s, sib_r, loc_s,
+    ag_s, ag_r, fw_s, fw_r, sib_s, sib_r, ready,
 ):
     n = tp // 2
-    blk = part.shape[1]
+    blk = stage.shape[1]
     cols = wbuf.shape[2]
     sub = blk // NS
     me = lax.axis_index("tp")
@@ -42,6 +44,24 @@
             src_ref=src, dst_ref=dst, send_sem=ss, recv_sem=rs,
             device_id={"tp": dev}, device_id_type=MESH,
         )
+
+    def part_row(job, q, k):
+        pair = job // 2
+        dq = jnp.where(pair == 0, -1, jnp.where(pair == 3, 0, 1))
+        kk = jnp.where(pair == 2, 1 - k, k)
+        return row_of(lax.rem(q + dq + n, n), kk, job - 2 * pair)
+
+    def recv_row(job, q, k):
+        pair = job // 2
+        dq = jnp.where(pair == 0, 0, jnp.where(pair == 1, 2, -1))
+        kk = jnp.where(pair == 1, k, 1 - k)
+        return row_of(lax.rem(q + dq + n, n), kk, job - 2 * pair)
+
+    def part(job, s, size):
+        return pl.ds(pl.multiple_of(part_row(job, chip, core) + s, size), size)
+
+    def recv(job, s, size):
+        return pl.ds(pl.multiple_of(recv_row(job, chip, core) + s, size), size)
 
     def load_x(pair):
         res = []
@@ -67,9 +87,6 @@
     def col(c):
         return pl.ds(pl.multiple_of(c * cols, cols), cols)
 
-    def row(s):
-        return pl.ds(pl.multiple_of(s * sub, sub), sub)
-
     for cp in load_x(0):
         cp.start()
     for c in range(NC):
@@ -99,16 +116,19 @@
     def pair_copy(t):
         pair, c, side = split(t)
         return remote(
-            stage.at[lax.rem(t, 4)], part.at[2 * pair + side, :, col(c)],
+            stage.at[lax.rem(t, 4)],
+            out.at[pl.ds(part_row(2 * pair + side, chip, 1 - core), blk), col(c)],
             pair_s.at[lax.rem(t, 4)], pair_r.at[t], sib,
         )
 
     def rs_copy(t):
         pair, c, side = split(t)
         job = 2 * pair + side
-        return remote(
-            part.at[job, :, col(c)], recv.at[job, :, col(c)],
-            rs_s.at[t], rs_r.at[t], jnp.where(side == 0, right, left),
+        to = chip_at(1 - 2 * side)
+        return remote(
+            out.at[part(job, 0, blk), col(c)],
+            out.at[pl.ds(recv_row(job, to, core), blk), col(c)],
+            rs_s.at[t], rs_r.at[t], 2 * to + core,
         )
 
     def product(pair, side, which, c):
@@ -146,8 +166,8 @@
             job = 2 * pair + side
             pair_copy(u).wait_recv()
             acc = product(pair, side, 0, c)
-            acc = acc + part[job, :, col(c)].astype(jnp.float32)
-            part[job, :, col(c)] = acc.astype(jnp.bfloat16)
+            acc = acc + out[part(job, 0, blk), col(c)].astype(jnp.float32)
+            out[part(job, 0, blk), col(c)] = acc.astype(jnp.bfloat16)
 
             @pl.when(u < 2 * per)
             def _():
@@ -161,9 +181,11 @@
     def cb_copy(i):
         s = i // 2
         side = i - 2 * s
-        return remote(
-            part.at[4 + side, row(s), :], recv.at[4 + side, row(s), :],
-            cb_s.at[i], cb_r.at[i], jnp.where(side == 0, right, left),
+        to = chip_at(1 - 2 * side)
+        dst = pl.multiple_of(recv_row(4 + side, to, core) + s * sub, sub)
+        return remote(
+            out.at[part(4 + side, s * sub, sub), :], out.at[pl.ds(dst, sub), :],
+            cb_s.at[i], cb_r.at[i], 2 * to + core,
         )
 
     @pl.loop(0, per)
@@ -174,10 +196,22 @@
     def _(i):
         s = i // 2
         side = i - 2 * s
-        total = part[4 + side, row(s), :].astype(jnp.float32)
-        total = total + recv[side, row(s), :].astype(jnp.float32)
-        part[4 + side, row(s), :] = total.astype(jnp.bfloat16)
+        total = out[part(4 + side, s * sub, sub), :].astype(jnp.float32)
+        total = total + out[recv(side, s * sub, sub), :].astype(jnp.float32)
+        out[part(4 + side, s * sub, sub), :] = total.astype(jnp.bfloat16)
         cb_copy(i).start()
+
+    def tell_ready(which):
+        for dev in (sib, left, right):
+            pl.semaphore_signal(
+                ready.at[which], inc=1, device_id={"tp": dev}, device_id_type=MESH
+            )
+
+    @pl.loop(0, 2 * per)
+    def _(t):
+        rs_copy(t).wait_send()
+
+    tell_ready(0)
 
     @pl.loop(per, 2 * per)
     def _(t):
@@ -185,6 +219,7 @@
 
     load_r.wait()
     load_g.wait()
+    pl.semaphore_wait(ready.at[0], 3)
 
     def out_rows(q, o, s, k=None):
         k = core if k is None else k
@@ -194,7 +229,7 @@
         s = i // 2
         o = i - 2 * s
         return remote(
-            part.at[6 + o, row(s), :], out_rows(chip, o, s),
+            out_rows(chip, o, s), out_rows(chip, o, s),
             ag_s.at[d, i], ag_r.at[d, i], right if d == 0 else left,
         )
 
@@ -202,14 +237,9 @@
         s = i // 2
         o = i - 2 * s
         return remote(
-            part.at[6 + o, row(s), :], out_rows(chip, o, s),
+            out_rows(chip, o, s), out_rows(chip, o, s),
             sib_s.at[0, i], sib_r.at[0, i], sib,
         )
-
-    def own_out(i):
-        s = i // 2
-        o = i - 2 * s
-        return pltpu.make_async_copy(part.at[6 + o, row(s), :], out_rows(chip, o, s), loc_s.at[i])
 
     grp = 16 if sub % 16 == 0 else sub
 
@@ -221,20 +251,26 @@
 
         @pl.loop(0, sub // grp)
         def _(b):
-            rows = pl.ds(pl.multiple_of(s * sub + b * grp, grp), grp)
-            y = part[6 + o, rows, :].astype(jnp.float32)
-            y = y + recv[2 + o, rows, :].astype(jnp.float32)
-            y = y + recv[5 - o, rows, :].astype(jnp.float32)
-            rr = rbuf[pl.ds(pl.multiple_of(o * blk + s * sub + b * grp, grp), grp), :]
+            at = s * sub + b * grp
+            y = out[part(6 + o, at, grp), :].astype(jnp.float32)
+            y = y + out[recv(2 + o, at, grp), :].astype(jnp.float32)
+            y = y + out[recv(5 - o, at, grp), :].astype(jnp.float32)
+            rr = rbuf[pl.ds(pl.multiple_of(o * blk + at, grp), grp), :]
             a = rr.astype(jnp.float32) + y.astype(jnp.bfloat16).astype(jnp.float32)
             ms = jnp.mean(a * a, axis=-1, keepdims=True)
-            z = a * lax.rsqrt(ms + EPS) * gbuf[...].astype(jnp.float32)
-            part[6 + o, rows, :] = z.astype(jnp.bfloat16)
+            z = a * lax.rsqrt(ms + EPS) * gbuf[...].astype(jnp.float32).reshape(1, -1)
+            out[part(6 + o, at, grp), :] = z.astype(jnp.bfloat16)
 
         ag_copy(i, 0).start()
         ag_copy(i, 1).start()
         own_sib(i).start()
-        own_out(i).start()
+
+    @pl.loop(0, 2 * NS)
+    def _(i):
+        cb_copy(i).wait_send()
+
+    tell_ready(1)
+    pl.semaphore_wait(ready.at[1], 3)
 
     def sib_copy(d, i):
         s = i // 2
@@ -271,14 +307,8 @@
     def _(t):
         pair_copy(t).wait_send()
 
-    @pl.loop(0, 2 * per)
-    def _(t):
-        rs_copy(t).wait_send()
-
     @pl.loop(0, 2 * NS)
     def _(i):
-        cb_copy(i).wait_send()
-        own_out(i).wait()
         own_sib(i).wait()
         for d in range(2):
             ag_copy(i, d).wait_send()
@@ -289,6 +319,18 @@
         for d in range(2):
             fw_copy(d, s).wait_send()
             fw_sib(d, s).wait()
+
+
+def write_out(z, o, sem):
+    rows = z.shape[0] // sem.shape[0]
+    copies = [
+        pltpu.make_async_copy(z.at[pl.ds(i * rows, rows), :], o.at[pl.ds(i * rows, rows), :], sem.at[i])
+        for i in range(sem.shape[0])
+    ]
+    for cp in copies:
+        cp.start()
+    for cp in copies:
+        cp.wait()
 
 
 def solution(mesh):
@@ -301,19 +343,17 @@
         dma = pltpu.SemaphoreType.DMA
         bf16 = jnp.bfloat16
         any_spec = pl.BlockSpec(memory_space=pl.ANY)
-        return pl.pallas_call(
+        z = pl.pallas_call(
             functools.partial(kernel, tp),
-            out_shape=jax.ShapeDtypeStruct((t, h), bf16),
+            out_shape=pltpu.VMEM((t, h), bf16),
             in_specs=[any_spec] * 4,
-            out_specs=any_spec,
+            out_specs=pl.BlockSpec(memory_space=pltpu.VMEM),
             scratch_shapes=[
                 pltpu.VMEM((2, 4, blk, f), bf16),
                 pltpu.VMEM((NC, f, h // NC), bf16),
-                pltpu.VMEM((1, h), bf16),
+                pltpu.VMEM((h,), bf16),
                 pltpu.VMEM((2 * blk, h), bf16),
                 pltpu.VMEM((4, blk, h // NC), bf16),
-                pltpu.VMEM((8, blk, h), bf16),
-                pltpu.VMEM((6, blk, h), bf16),
                 dma((2, 4)), dma((NC,)), dma((2,)),
                 dma((4,)), dma((8 * NC,)),
                 dma((4 * NC,)), dma((4 * NC,)),
@@ -321,15 +361,23 @@
                 dma((2, 2 * NS)), dma((2, 2 * NS)),
                 dma((2, NS)), dma((2, NS)),
                 dma((4, 2 * NS)), dma((4, 2 * NS)),
-                dma((2 * NS,)),
+                pltpu.SemaphoreType.REGULAR((2,)),
             ],
             compiler_params=pltpu.CompilerParams(
-                collective_id=0, has_side_effects=True, vmem_limit_bytes=67043328,
+                collective_id=0, has_side_effects=True, vmem_limit_bytes=VMEM_COMM,
             ),
             cost_estimate=pl.CostEstimate(
-                flops=2 * t * f * h, bytes_accessed=2 * (t * f + f * h + 3 * t * h), transcendentals=0
+                flops=2 * t * f * h, bytes_accessed=2 * (t * f + f * h + 2 * t * h), transcendentals=0
             ),
-        )(x, w, r, g.reshape(1, h))
+        )(x, w, r, g)
+        return pl.pallas_call(
+            write_out,
+            out_shape=jax.ShapeDtypeStruct((t, h), bf16),
+            in_specs=[pl.BlockSpec(memory_space=pltpu.VMEM)],
+            out_specs=any_spec,
+            scratch_shapes=[dma((16,))],
+            compiler_params=pltpu.CompilerParams(vmem_limit_bytes=VMEM_WRITE),
+        )(z)
 
     return jax.shard_map(
         local,

time: 311 us -> 298 us (0.958)
  local copies, waits for them, and re-layouts: 24.2 us -> 0 us
  Pallas kernels: 287 us -> 298 us
    unnamed x1 -> x0, local copies, waits for them, and re-layouts: 22.9 us -> none
    pallas_call x1 -> x2, Pallas kernels: 287 us -> 298 us  [the longest x1 287 us: local(): pl.pallas_call(functools.partial(kernel, tp), out_shape=pltpu.VMEM((t, h)...]
where the time goes in v2:
time: 298 us
  Pallas kernels  298 us (100%)
    pallas_call x1, Pallas kernels, local(): pl.pallas_call(functools.partial(kernel, tp), out_shape=pltpu.VMEM((t, h)...  287 us
    pallas_call x1, Pallas kernels, local(): pl.pallas_call(write_out, out_shape=jax.ShapeDtypeStruct((t, h), bf16), i...  11 us

profile of v2, /device:TPU:81, one launch (start us, length us, event | category | flops | bytes accessed | tf_op | source)
XLA Modules:
  0.0 297.6 jit_solution(3881140996507599216)
XLA Ops:
  0.0 286.5 %shard_map.46.z = bf16[4096,4096]{1,0:T(8,128)(2,1)S(1)} custom-call(bf16[4096,1792]{1,0:T(8,128)(2,1)} %x.1, bf16[1792,4096]{1,0:T(8,128)(2,1)} %w.1, bf16[4096,4096]{1,0:T(8,128)(2,1)} %r.1, bf16[4096]{0:T(1024)(128)(2,1)} %g.1), custom_call_target="tpu_custom_call" | custom-call | flops 60129542144 | bytes 96468992 | tf_op jit(solution)/shard_map/pallas_call | solution.py:346
  286.6 11.0 %shard_map.47 = bf16[4096,4096]{1,0:T(8,128)(2,1)} custom-call(bf16[4096,4096]{1,0:T(8,128)(2,1)S(1)} %shard_map.46.z), custom_call_target="tpu_custom_call" | custom-call | tf_op jit(solution)/shard_map/pallas_call | solution.py:373

commit v3 on v2

--- a/solution.py
+++ b/solution.py
@@ -9,7 +9,7 @@
 
 EPS = 1e-6
 MESH = pl.DeviceIdType.MESH
-NC = 4
+NC = 8
 NS = 4
 VMEM_COMM = 30 * 1024 * 1024
 VMEM_WRITE = 1024 * 1024
@@ -19,10 +19,10 @@
     tp, x, w, r, g, out,
     xbuf, wbuf, gbuf, rbuf, stage,
     x_sem, w_sem, g_sem, pair_s, pair_r, rs_s, rs_r, cb_s, cb_r,
-    ag_s, ag_r, fw_s, fw_r, sib_s, sib_r, ready,
+    ag_s, ag_r, fw_s, fw_r, ts_s, ts_r, sib_s, sib_r, ready,
 ):
     n = tp // 2
-    blk = stage.shape[1]
+    blk = stage.shape[1] // 2
     cols = wbuf.shape[2]
     sub = blk // NS
     me = lax.axis_index("tp")
@@ -63,21 +63,16 @@
     def recv(job, s, size):
         return pl.ds(pl.multiple_of(recv_row(job, chip, core) + s, size), size)
 
-    def load_x(pair):
-        res = []
-        for side in range(2):
-            sign = 1 - 2 * side
-            q = chip_at(sign * ((4 - pair) // 2))
-            o = lax.rem(side + 1 + pair, 2)
-            for which in range(2):
-                k = core if which == 0 else 1 - core
-                slot = lax.rem(pair, 2)
-                res.append(pltpu.make_async_copy(
-                    x.at[pl.ds(row_of(q, k, o), blk), :],
-                    xbuf.at[slot, 2 * side + which],
-                    x_sem.at[slot, 2 * side + which],
-                ))
-        return res
+    def load_x(pair, side, which):
+        q = chip_at((1 - 2 * side) * ((4 - pair) // 2))
+        o = lax.rem(side + 1 + pair, 2)
+        k = core if which == 0 else 1 - core
+        slot = lax.rem(pair, 2)
+        return pltpu.make_async_copy(
+            x.at[pl.ds(row_of(q, k, o), blk), :],
+            xbuf.at[slot, which, pl.ds(side * blk, blk), :],
+            x_sem.at[slot, which, side],
+        )
 
     def load_w(c):
         return pltpu.make_async_copy(
@@ -87,96 +82,198 @@
     def col(c):
         return pl.ds(pl.multiple_of(c * cols, cols), cols)
 
-    for cp in load_x(0):
-        cp.start()
-    for c in range(NC):
-        load_w(c).start()
-    for cp in load_x(1):
-        cp.start()
+    def start_x(pair, which):
+        for side in range(2):
+            load_x(pair, side, which).start()
+
+    def wait_x(pair, which):
+        for side in range(2):
+            load_x(pair, side, which).wait()
+
+    pieces = ((0, cols // 4), (cols // 4, cols - cols // 4))
+
+    def load_w0(i):
+        at, size = pieces[i]
+        return pltpu.make_async_copy(
+            w.at[:, pl.ds(at, size)], wbuf.at[0, :, pl.ds(at, size)], w_sem.at[i * NC]
+        )
+
+    start_x(0, 1)
+    load_w0(0).start()
+    start_x(0, 0)
+    load_w0(1).start()
+    load_w(1).start()
     own0 = row_of(chip, core, 0)
     load_r = pltpu.make_async_copy(r.at[pl.ds(own0, 2 * blk), :], rbuf, g_sem.at[0])
     load_g = pltpu.make_async_copy(g, gbuf, g_sem.at[1])
-    load_r.start()
-    load_g.start()
 
     barrier = pltpu.get_barrier_semaphore()
     for dev in (sib, left, right):
         pl.semaphore_signal(barrier, inc=1, device_id={"tp": dev}, device_id_type=MESH)
+
+    steps = 4 * NC
+
+    def pair_copy(t, side):
+        pair = t // NC
+        slot = lax.rem(t, 4)
+        return remote(
+            stage.at[slot, pl.ds(side * blk, blk), :],
+            out.at[pl.ds(part_row(2 * pair + side, chip, 1 - core), blk), col(t - pair * NC)],
+            pair_s.at[slot, side], pair_r.at[t, side], sib,
+        )
+
+    def far_copy(c, side):
+        to = chip_at(1 - 2 * side)
+        return remote(
+            out.at[part(side, 0, blk), col(c)],
+            out.at[pl.ds(recv_row(side, to, core), blk), col(c)],
+            rs_s.at[side, c], rs_r.at[side, c], 2 * to + core,
+        )
+
+    def near_copy(side):
+        to = chip_at(1 - 2 * side)
+        return remote(
+            out.at[part(2 + side, 0, blk), :],
+            out.at[pl.ds(recv_row(2 + side, to, core), blk), :],
+            rs_s.at[side, NC], rs_r.at[side, NC], 2 * to + core,
+        )
+
+    def product(pair, which, c):
+        return jnp.dot(
+            xbuf[lax.rem(pair, 2), which], wbuf[c], preferred_element_type=jnp.float32
+        )
+
+    def give(t):
+        pair = t // NC
+        stage[lax.rem(t, 4)] = product(pair, 1, t - pair * NC).astype(jnp.bfloat16)
+
+    def start_give(t):
+        for side in range(2):
+            pair_copy(t, side).start()
+
+    def take(t):
+        pair = t // NC
+        c = t - pair * NC
+        acc = product(pair, 0, c)
+        for side in range(2):
+            pair_copy(t, side).wait_recv()
+            rows = part(2 * pair + side, 0, blk)
+            both = acc[side * blk:(side + 1) * blk] + out[rows, col(c)].astype(jnp.float32)
+            out[rows, col(c)] = both.astype(jnp.bfloat16)
+
+            @pl.when(pair == 0)
+            def _():
+                far_copy(c, side).start()
+
+            @pl.when(jnp.logical_and(pair == 1, c == NC - 1))
+            def _():
+                near_copy(side).start()
+
+    def first_pair(i, side):
+        at, size = pieces[i]
+        return remote(
+            stage.at[0, pl.ds(side * blk, blk), pl.ds(at, size)],
+            out.at[pl.ds(part_row(side, chip, 1 - core), blk), pl.ds(at, size)],
+            pair_s.at[4 * i, side], pair_r.at[i * steps, side], sib,
+        )
+
+    def first_far(i, side):
+        at, size = pieces[i]
+        to = chip_at(1 - 2 * side)
+        return remote(
+            out.at[part(side, 0, blk), pl.ds(at, size)],
+            out.at[pl.ds(recv_row(side, to, core), blk), pl.ds(at, size)],
+            rs_s.at[side, i * (NC + 1)], rs_r.at[side, i * (NC + 1)], 2 * to + core,
+        )
+
+    def first_product(i, which):
+        at, size = pieces[i]
+        return jnp.dot(
+            xbuf[0, which], wbuf[0, :, at:at + size], preferred_element_type=jnp.float32
+        )
+
+    def first_give(i):
+        at, size = pieces[i]
+        stage[0, :, at:at + size] = first_product(i, 1).astype(jnp.bfloat16)
+
+    def first_take(i, acc):
+        at, size = pieces[i]
+        for side in range(2):
+            first_pair(i, side).wait_recv()
+            rows = part(side, 0, blk)
+            there = out[rows, at:at + size].astype(jnp.float32)
+            out[rows, at:at + size] = (acc[side * blk:(side + 1) * blk] + there).astype(jnp.bfloat16)
+            first_far(i, side).start()
+
+    wait_x(0, 1)
+    load_w0(0).wait()
+    first_give(0)
     pl.semaphore_wait(barrier, 3)
-
-    per = 2 * NC
-    steps = 4 * per
-
-    def split(t):
-        pair = t // per
-        c = (t - pair * per) // 2
-        side = t - 2 * (t // 2)
-        return pair, c, side
-
-    def pair_copy(t):
-        pair, c, side = split(t)
-        return remote(
-            stage.at[lax.rem(t, 4)],
-            out.at[pl.ds(part_row(2 * pair + side, chip, 1 - core), blk), col(c)],
-            pair_s.at[lax.rem(t, 4)], pair_r.at[t], sib,
-        )
-
-    def rs_copy(t):
-        pair, c, side = split(t)
-        job = 2 * pair + side
-        to = chip_at(1 - 2 * side)
-        return remote(
-            out.at[part(job, 0, blk), col(c)],
-            out.at[pl.ds(recv_row(job, to, core), blk), col(c)],
-            rs_s.at[t], rs_r.at[t], 2 * to + core,
-        )
-
-    def product(pair, side, which, c):
-        return jnp.dot(
-            xbuf[lax.rem(pair, 2), 2 * side + which], wbuf[c],
-            preferred_element_type=jnp.float32,
-        )
-
-    @pl.loop(0, steps + 1)
+    for side in range(2):
+        first_pair(0, side).start()
+    wait_x(0, 0)
+    acc = first_product(0, 0)
+    load_w0(1).wait()
+    load_w(2).start()
+    first_give(1)
+    for side in range(2):
+        first_pair(1, side).start()
+    first_take(0, acc)
+    first_take(1, first_product(1, 0))
+    for i in range(2):
+        for side in range(2):
+            first_pair(i, side).wait_send()
+
+    @pl.loop(1, steps + 1)
     def _(t):
         @pl.when(t < steps)
         def _():
-            pair, c, side = split(t)
-
-            @pl.when(lax.rem(t, per) == 0)
-            def _():
-                for cp in load_x(pair):
-                    cp.wait()
-
-            @pl.when(jnp.logical_and(t < per, side == 0))
+            pair = t // NC
+            c = t - pair * NC
+
+            @pl.when(c == 0)
+            def _():
+                wait_x(pair, 1)
+
+            @pl.when(t < NC)
             def _():
                 load_w(c).wait()
 
-            @pl.when(t >= 4)
-            def _():
-                pair_copy(t - 4).wait_send()
-
-            stage[lax.rem(t, 4)] = product(pair, side, 1, c).astype(jnp.bfloat16)
-            pair_copy(t).start()
-
-        @pl.when(t > 0)
+            @pl.when(t < NC - 2)
+            def _():
+                load_w(c + 2).start()
+
+            @pl.when(t == NC // 2)
+            def _():
+                start_x(1, 1)
+                start_x(1, 0)
+                load_r.start()
+                load_g.start()
+
+            @pl.when(t > 4)
+            def _():
+                for side in range(2):
+                    pair_copy(t - 4, side).wait_send()
+
+            give(t)
+            start_give(t)
+
+        @pl.when(t > 1)
         def _():
             u = t - 1
-            pair, c, side = split(u)
-            job = 2 * pair + side
-            pair_copy(u).wait_recv()
-            acc = product(pair, side, 0, c)
-            acc = acc + out[part(job, 0, blk), col(c)].astype(jnp.float32)
-            out[part(job, 0, blk), col(c)] = acc.astype(jnp.bfloat16)
-
-            @pl.when(u < 2 * per)
-            def _():
-                rs_copy(u).start()
-
-            @pl.when(jnp.logical_and(lax.rem(u, per) == per - 1, pair < 2))
-            def _():
-                for cp in load_x(pair + 2):
-                    cp.start()
+            pair = u // NC
+            c = u - pair * NC
+
+            @pl.when(c == 0)
+            def _():
+                wait_x(pair, 0)
+
+            take(u)
+
+            @pl.when(jnp.logical_and(c == NC - 1, pair < 2))
+            def _():
+                start_x(pair + 2, 1)
+                start_x(pair + 2, 0)
 
     def cb_copy(i):
         s = i // 2
@@ -188,9 +285,14 @@
             cb_s.at[i], cb_r.at[i], 2 * to + core,
         )
 
-    @pl.loop(0, per)
-    def _(t):
-        rs_copy(t).wait_recv()
+    for i in range(2):
+        for side in range(2):
+            first_far(i, side).wait_recv()
+
+    @pl.loop(1, NC)
+    def _(c):
+        for side in range(2):
+            far_copy(c, side).wait_recv()
 
     @pl.loop(0, 2 * NS)
     def _(i):
@@ -207,15 +309,27 @@
                 ready.at[which], inc=1, device_id={"tp": dev}, device_id_type=MESH
             )
 
-    @pl.loop(0, 2 * per)
+    for i in range(2):
+        for side in range(2):
+            first_far(i, side).wait_send()
+
+    @pl.loop(1, NC)
+    def _(c):
+        for side in range(2):
+            far_copy(c, side).wait_send()
+
+    for side in range(2):
+        near_copy(side).wait_send()
+
+    @pl.loop(steps - 4, steps)
     def _(t):
-        rs_copy(t).wait_send()
+        for side in range(2):
+            pair_copy(t, side).wait_send()
 
     tell_ready(0)
 
-    @pl.loop(per, 2 * per)
-    def _(t):
-        rs_copy(t).wait_recv()
+    for side in range(2):
+        near_copy(side).wait_recv()
 
     load_r.wait()
     load_g.wait()
@@ -278,34 +392,34 @@
         rows = out_rows(chip_at(-1 if d == 0 else 1), o, s)
         return remote(rows, rows, sib_s.at[1 + d, i], sib_r.at[1 + d, i], sib)
 
-    def fw_copy(d, s):
-        rows = out_rows(chip_at(-1 if d == 0 else 1), d, s)
-        return remote(rows, rows, fw_s.at[d, s], fw_r.at[d, s], right if d == 0 else left)
-
-    def fw_sib(d, s):
-        rows = out_rows(chip_at(2), d, s)
-        return remote(rows, rows, sib_s.at[3, 2 * s + d], sib_r.at[3, 2 * s + d], sib)
-
-    @pl.loop(0, NS)
-    def _(s):
+    tail = [(s * sub, sub) for s in range(NS - 1)]
+    tail += [(blk - sub, sub // 2), (blk - sub // 2, sub // 4), (blk - sub // 4, sub // 4)]
+
+    def fw_rows(q, d, p):
+        at, size = tail[p]
+        return out.at[pl.ds(pl.multiple_of(row_of(q, core, d) + at, size), size), :]
+
+    def fw_copy(d, p):
+        rows = fw_rows(chip_at(-1 if d == 0 else 1), d, p)
+        return remote(rows, rows, fw_s.at[d, p], fw_r.at[d, p], right if d == 0 else left)
+
+    def fw_in(d, p):
+        rows = fw_rows(chip_at(2), d, p)
+        return remote(rows, rows, fw_s.at[d, p], fw_r.at[d, p], sib)
+
+    def fw_sib(d, p):
+        rows = fw_rows(chip_at(2), d, p)
+        return remote(rows, rows, ts_s.at[d, p], ts_r.at[d, p], sib)
+
+    for s in range(NS):
         for o in range(2):
             i = 2 * s + o
             for d in range(2):
                 ag_copy(i, d).wait_recv()
                 if o == d:
-                    fw_copy(d, s).start()
+                    for p in range(s, len(tail) if s == NS - 1 else s + 1):
+                        fw_copy(d, p).start()
                 sib_copy(d, i).start()
-
-    @pl.loop(0, NS)
-    def _(s):
-        for d in range(2):
-            rows = out_rows(chip_at(2), d, s)
-            remote(rows, rows, fw_s.at[d, s], fw_r.at[d, s], sib).wait_recv()
-            fw_sib(d, s).start()
-
-    @pl.loop(steps - 4, steps)
-    def _(t):
-        pair_copy(t).wait_send()
 
     @pl.loop(0, 2 * NS)
     def _(i):
@@ -314,11 +428,16 @@
             ag_copy(i, d).wait_send()
             sib_copy(d, i).wait()
 
-    @pl.loop(0, NS)
-    def _(s):
+    for p in range(len(tail)):
         for d in range(2):
-            fw_copy(d, s).wait_send()
-            fw_sib(d, s).wait()
+            fw_in(d, p).wait_recv()
+            fw_sib(d, p).start()
+            fw_copy(d, p).wait_send()
+            if p:
+                fw_sib(d, p - 1).wait()
+
+    for d in range(2):
+        fw_sib(d, len(tail) - 1).wait()
 
 
 def write_out(z, o, sem):
@@ -349,18 +468,19 @@
             in_specs=[any_spec] * 4,
             out_specs=pl.BlockSpec(memory_space=pltpu.VMEM),
             scratch_shapes=[
-                pltpu.VMEM((2, 4, blk, f), bf16),
+                pltpu.VMEM((2, 2, 2 * blk, f), bf16),
                 pltpu.VMEM((NC, f, h // NC), bf16),
                 pltpu.VMEM((h,), bf16),
                 pltpu.VMEM((2 * blk, h), bf16),
-                pltpu.VMEM((4, blk, h // NC), bf16),
-                dma((2, 4)), dma((NC,)), dma((2,)),
-                dma((4,)), dma((8 * NC,)),
-                dma((4 * NC,)), dma((4 * NC,)),
+                pltpu.VMEM((4, 2 * blk, h // NC), bf16),
+                dma((2, 2, 2)), dma((NC + 1,)), dma((2,)),
+                dma((5, 2)), dma((4 * NC + 1, 2)),
+                dma((2, NC + 2)), dma((2, NC + 2)),
                 dma((2 * NS,)), dma((2 * NS,)),
                 dma((2, 2 * NS)), dma((2, 2 * NS)),
-                dma((2, NS)), dma((2, NS)),
-                dma((4, 2 * NS)), dma((4, 2 * NS)),
+                dma((2, NS + 2)), dma((2, NS + 2)),
+                dma((2, NS + 2)), dma((2, NS + 2)),
+                dma((3, 2 * NS)), dma((3, 2 * NS)),
                 pltpu.SemaphoreType.REGULAR((2,)),
             ],
             compiler_params=pltpu.CompilerParams(

time: 298 us -> 295 us (0.990)
  Pallas kernels: 298 us -> 295 us
where the time goes in v3:
time: 295 us
  Pallas kernels  295 us (100%)
    pallas_call x1, Pallas kernels, local(): pl.pallas_call(functools.partial(kernel, tp), out_shape=pltpu.VMEM((t, h)...  284 us
    pallas_call x1, Pallas kernels, local(): pl.pallas_call(write_out, out_shape=jax.ShapeDtypeStruct((t, h), bf16), i...  11 us

profile of v3, /device:TPU:81, one launch (start us, length us, event | category | flops | bytes accessed | tf_op | source)
XLA Modules:
  0.0 294.7 jit_solution(15363663280449927724)
XLA Ops:
  0.0 283.7 %shard_map.46.z = bf16[4096,4096]{1,0:T(8,128)(2,1)S(1)} custom-call(bf16[4096,1792]{1,0:T(8,128)(2,1)} %x.1, bf16[1792,4096]{1,0:T(8,128)(2,1)} %w.1, bf16[4096,4096]{1,0:T(8,128)(2,1)} %r.1, bf16[4096]{0:T(1024)(128)(2,1)} %g.1), custom_call_target="tpu_custom_call" | custom-call | flops 60129542144 | bytes 96468992 | tf_op jit(solution)/shard_map/pallas_call | solution.py:465
  283.7 11.0 %shard_map.47 = bf16[4096,4096]{1,0:T(8,128)(2,1)} custom-call(bf16[4096,4096]{1,0:T(8,128)(2,1)S(1)} %shard_map.46.z), custom_call_target="tpu_custom_call" | custom-call | tf_op jit(solution)/shard_map/pallas_call | solution.py:493

commit v4 on v3

--- a/solution.py
+++ b/solution.py
@@ -90,7 +90,7 @@
         for side in range(2):
             load_x(pair, side, which).wait()
 
-    pieces = ((0, cols // 4), (cols // 4, cols - cols // 4))
+    pieces = ((0, cols // 2), (cols // 2, cols - cols // 2))
 
     def load_w0(i):
         at, size = pieces[i]
@@ -212,13 +212,12 @@
     for side in range(2):
         first_pair(0, side).start()
     wait_x(0, 0)
-    acc = first_product(0, 0)
+    first_take(0, first_product(0, 0))
     load_w0(1).wait()
     load_w(2).start()
     first_give(1)
     for side in range(2):
         first_pair(1, side).start()
-    first_take(0, acc)
     first_take(1, first_product(1, 0))
     for i in range(2):
         for side in range(2):
@@ -393,7 +392,8 @@
         return remote(rows, rows, sib_s.at[1 + d, i], sib_r.at[1 + d, i], sib)
 
     tail = [(s * sub, sub) for s in range(NS - 1)]
-    tail += [(blk - sub, sub // 2), (blk - sub // 2, sub // 4), (blk - sub // 4, sub // 4)]
+    tail += [(blk - sub, sub // 2), (blk - sub // 2, sub // 4)]
+    tail += [(blk - sub // 4, sub // 8), (blk - sub // 8, sub // 8)]
 
     def fw_rows(q, d, p):
         at, size = tail[p]
@@ -478,8 +478,8 @@
                 dma((2, NC + 2)), dma((2, NC + 2)),
                 dma((2 * NS,)), dma((2 * NS,)),
                 dma((2, 2 * NS)), dma((2, 2 * NS)),
-                dma((2, NS + 2)), dma((2, NS + 2)),
-                dma((2, NS + 2)), dma((2, NS + 2)),
+                dma((2, NS + 3)), dma((2, NS + 3)),
+                dma((2, NS + 3)), dma((2, NS + 3)),
                 dma((3, 2 * NS)), dma((3, 2 * NS)),
                 pltpu.SemaphoreType.REGULAR((2,)),
             ],

time: 295 us -> 294 us (level)
  no operation moved by 1% of the time
where the time goes in v4:
time: 294 us
  Pallas kernels  294 us (100%)
    pallas_call x1, Pallas kernels, local(): pl.pallas_call(functools.partial(kernel, tp), out_shape=pltpu.VMEM((t, h)...  283 us
    pallas_call x1, Pallas kernels, local(): pl.pallas_call(write_out, out_shape=jax.ShapeDtypeStruct((t, h), bf16), i...  11 us

profile of v4, /device:TPU:81, one launch (start us, length us, event | category | flops | bytes accessed | tf_op | source)
XLA Modules:
  0.0 294.3 jit_solution(971619431399557110)
XLA Ops:
  0.0 283.2 %shard_map.46.z = bf16[4096,4096]{1,0:T(8,128)(2,1)S(1)} custom-call(bf16[4096,1792]{1,0:T(8,128)(2,1)} %x.1, bf16[1792,4096]{1,0:T(8,128)(2,1)} %w.1, bf16[4096,4096]{1,0:T(8,128)(2,1)} %r.1, bf16[4096]{0:T(1024)(128)(2,1)} %g.1), custom_call_target="tpu_custom_call" | custom-call | flops 60129542144 | bytes 96468992 | tf_op jit(solution)/shard_map/pallas_call | solution.py:465
  283.3 11.0 %shard_map.47 = bf16[4096,4096]{1,0:T(8,128)(2,1)} custom-call(bf16[4096,4096]{1,0:T(8,128)(2,1)S(1)} %shard_map.46.z), custom_call_target="tpu_custom_call" | custom-call | tf_op jit(solution)/shard_map/pallas_call | solution.py:493

commit v5 on v4

--- a/solution.py
+++ b/solution.py
@@ -334,25 +334,18 @@
     load_g.wait()
     pl.semaphore_wait(ready.at[0], 3)
 
-    def out_rows(q, o, s, k=None):
-        k = core if k is None else k
-        return out.at[pl.ds(pl.multiple_of(row_of(q, k, o) + s * sub, sub), sub), :]
+    def two_chunks(q, i):
+        half = i // 2
+        row = row_of(q, core, i - 2 * half) + half * 2 * sub
+        return out.at[pl.ds(pl.multiple_of(row, 2 * sub), 2 * sub), :]
 
     def ag_copy(i, d):
-        s = i // 2
-        o = i - 2 * s
-        return remote(
-            out_rows(chip, o, s), out_rows(chip, o, s),
-            ag_s.at[d, i], ag_r.at[d, i], right if d == 0 else left,
-        )
+        rows = two_chunks(chip, i)
+        return remote(rows, rows, ag_s.at[d, i], ag_r.at[d, i], right if d == 0 else left)
 
     def own_sib(i):
-        s = i // 2
-        o = i - 2 * s
-        return remote(
-            out_rows(chip, o, s), out_rows(chip, o, s),
-            sib_s.at[0, i], sib_r.at[0, i], sib,
-        )
+        rows = two_chunks(chip, i)
+        return remote(rows, rows, sib_s.at[0, i], sib_r.at[0, i], sib)
 
     grp = 16 if sub % 16 == 0 else sub
 
@@ -374,9 +367,12 @@
             z = a * lax.rsqrt(ms + EPS) * gbuf[...].astype(jnp.float32).reshape(1, -1)
             out[part(6 + o, at, grp), :] = z.astype(jnp.bfloat16)
 
-        ag_copy(i, 0).start()
-        ag_copy(i, 1).start()
-        own_sib(i).start()
+        @pl.when(s - 2 * (s // 2) == 1)
+        def _():
+            done = s - 1 + o
+            ag_copy(done, 0).start()
+            ag_copy(done, 1).start()
+            own_sib(done).start()
 
     @pl.loop(0, 2 * NS)
     def _(i):
@@ -386,9 +382,7 @@
     pl.semaphore_wait(ready.at[1], 3)
 
     def sib_copy(d, i):
-        s = i // 2
-        o = i - 2 * s
-        rows = out_rows(chip_at(-1 if d == 0 else 1), o, s)
+        rows = two_chunks(chip_at(-1 if d == 0 else 1), i)
         return remote(rows, rows, sib_s.at[1 + d, i], sib_r.at[1 + d, i], sib)
 
     tail = [(s * sub, sub) for s in range(NS - 1)]
@@ -411,17 +405,17 @@
         rows = fw_rows(chip_at(2), d, p)
         return remote(rows, rows, ts_s.at[d, p], ts_r.at[d, p], sib)
 
-    for s in range(NS):
+    for half in range(NS // 2):
         for o in range(2):
-            i = 2 * s + o
+            i = 2 * half + o
             for d in range(2):
                 ag_copy(i, d).wait_recv()
                 if o == d:
-                    for p in range(s, len(tail) if s == NS - 1 else s + 1):
+                    for p in range(2 * half, len(tail) if half else 2):
                         fw_copy(d, p).start()
                 sib_copy(d, i).start()
 
-    @pl.loop(0, 2 * NS)
+    @pl.loop(0, NS)
     def _(i):
         own_sib(i).wait()
         for d in range(2):
@@ -477,10 +471,10 @@
                 dma((5, 2)), dma((4 * NC + 1, 2)),
                 dma((2, NC + 2)), dma((2, NC + 2)),
                 dma((2 * NS,)), dma((2 * NS,)),
-                dma((2, 2 * NS)), dma((2, 2 * NS)),
+                dma((2, NS)), dma((2, NS)),
                 dma((2, NS + 3)), dma((2, NS + 3)),
                 dma((2, NS + 3)), dma((2, NS + 3)),
-                dma((3, 2 * NS)), dma((3, 2 * NS)),
+                dma((3, NS)), dma((3, NS)),
                 pltpu.SemaphoreType.REGULAR((2,)),
             ],
             compiler_params=pltpu.CompilerParams(

time: 294 us -> 294 us (level)
  no operation moved by 1% of the time
where the time goes in v5:
time: 294 us
  Pallas kernels  294 us (100%)
    pallas_call x1, Pallas kernels, local(): pl.pallas_call(functools.partial(kernel, tp), out_shape=pltpu.VMEM((t, h)...  283 us
    pallas_call x1, Pallas kernels, local(): pl.pallas_call(write_out, out_shape=jax.ShapeDtypeStruct((t, h), bf16), i...  11 us

profile of v5, /device:TPU:81, one launch (start us, length us, event | category | flops | bytes accessed | tf_op | source)
XLA Modules:
  0.0 293.9 jit_solution(11175347437706617655)
XLA Ops:
  0.0 282.9 %shard_map.46.z = bf16[4096,4096]{1,0:T(8,128)(2,1)S(1)} custom-call(bf16[4096,1792]{1,0:T(8,128)(2,1)} %x.1, bf16[1792,4096]{1,0:T(8,128)(2,1)} %w.1, bf16[4096,4096]{1,0:T(8,128)(2,1)} %r.1, bf16[4096]{0:T(1024)(128)(2,1)} %g.1), custom_call_target="tpu_custom_call" | custom-call | flops 60129542144 | bytes 96468992 | tf_op jit(solution)/shard_map/pallas_call | solution.py:459
  282.9 11.0 %shard_map.47 = bf16[4096,4096]{1,0:T(8,128)(2,1)} custom-call(bf16[4096,4096]{1,0:T(8,128)(2,1)S(1)} %shard_map.46.z), custom_call_target="tpu_custom_call" | custom-call | tf_op jit(solution)/shard_map/pallas_call | solution.py:487
